TPU v7x, 32 devices: a whole 2x2x4 slice. The times are simulated.
32 devices in a mesh: rows: 16 (over z, y, x), feat: 2 (over core).
Axes of the slice: x: 2, y: 2, z: 4, core: 2. Of those that a mesh axis runs over, the one named last changes fastest.
Arguments:
- queries: bfloat16 [1024, 128], P('rows', 'feat'), may hold values from -6 to 6
- corpus: bfloat16 [524288, 128], P(('rows', 'feat')), as said below
- candidates: int32 [1024, 100], P(('rows', 'feat')), may hold values from 0 to 524287, as said below
- threshold: int32 [1024], replicated, may hold values from 100 to 199, as said below
Outputs:
- exceed: float32 [1024], P(('rows', 'feat'))
- candidate_scores: float32 [1024, 100], P(('rows', 'feat'))
Inputs may be any that keep to these rules, and one draw needn't show every extreme that they name: Passage ids. Of the 3200 candidates of one device's queries (aligned blocks of 32 rows), at most 100 lie in the 16384 passages of any one device, and exactly 100 in some device's. `corpus`: passage embeddings of order one or smaller; their scale differs between passages. Some query has threshold 100 and some 199.
All inputs are finite; a program needn't handle non-finite values.
Results may differ from a plain program's by a relative error of at most 0.00035.
Values may be sent and summed in bfloat16 or wider, within the bound.
A program may use at most 64 MiB of HBM per device.

v0:
```python
import jax
import jax.numpy as jnp
from jax import lax
from jax.sharding import PartitionSpec as P


def body(queries, corpus, candidates, threshold):
    rows_dev = corpus.shape[0]
    width = corpus.shape[1]
    shards = lax.axis_size("rows") * lax.axis_size("feat")
    owned_queries = candidates.shape[0]
    per_query = candidates.shape[1]
    npass_all = rows_dev * shards
    cutoff = threshold.astype(jnp.float32) * 0.01
    owner = lax.axis_index(("rows", "feat"))
    full_rows = lax.all_gather(queries, "feat", axis=1, tiled=True)
    whole = lax.all_gather(full_rows, "rows", axis=0, tiled=True)
    query_count = whole.shape[0]
    block = 2048
    corpus_blocks = corpus.reshape(rows_dev // block, block, width)

    def visit(total, block_rows):
        scores = lax.dot_general(
            whole, block_rows, (((1,), (1,)), ((), ())), preferred_element_type=jnp.float32
        )
        return (total + jnp.sum(jnp.maximum(scores - cutoff[:, None], 0.0), axis=1), None)

    total, _ = lax.scan(visit, jnp.zeros((query_count,), jnp.float32), corpus_blocks)
    flat_ids = candidates.reshape(-1)
    total_ids = flat_ids.shape[0]
    capacity = (total_ids + shards - 1) // shards
    target = flat_ids // rows_dev
    onehot = (target[:, None] == jnp.arange(shards, dtype=jnp.int32)[None, :]).astype(jnp.int32)
    before = jnp.cumsum(onehot, axis=0) - onehot
    rank = jnp.sum(before * onehot, axis=1)
    query_ids = owner * owned_queries + jnp.arange(total_ids, dtype=jnp.int32) // per_query
    fields = jnp.stack([flat_ids - target * rows_dev, query_ids], axis=1)
    send_both = jnp.zeros((shards, capacity, 2), jnp.int32).at[target, rank].set(fields)
    n_rows = lax.axis_size("rows")
    n_feat = lax.axis_size("feat")
    received = lax.all_to_all(
        lax.all_to_all(
            send_both.reshape(n_rows, n_feat, capacity * 2),
            "rows",
            split_axis=0,
            concat_axis=0,
            tiled=True,
        ),
        "feat",
        split_axis=1,
        concat_axis=1,
        tiled=True,
    )
    received = received.reshape(shards * capacity, 2)
    picked = corpus[received[:, 0]]
    asked = whole[received[:, 1]]
    values = jnp.einsum("kd,kd->k", picked, asked, preferred_element_type=jnp.float32).reshape(
        n_rows, n_feat, capacity
    )
    partials = total.reshape(n_rows, n_feat, owned_queries)
    answers, mass_parts = (
        lax.all_to_all(
            lax.all_to_all(values, "rows", split_axis=0, concat_axis=0, tiled=True),
            "feat",
            split_axis=1,
            concat_axis=1,
            tiled=True,
        ),
        lax.all_to_all(
            lax.all_to_all(partials, "rows", split_axis=0, concat_axis=0, tiled=True),
            "feat",
            split_axis=1,
            concat_axis=1,
            tiled=True,
        ),
    )
    exceed = jnp.sum(mass_parts, axis=(0, 1)) * (8.0 / npass_all)
    candidate_scores = answers.reshape(shards, capacity)[target, rank].reshape(
        owned_queries, per_query
    )
    return (exceed, candidate_scores)


def solution(mesh):
    return jax.shard_map(
        body,
        mesh=mesh,
        in_specs=(P("rows", "feat"), P(("rows", "feat"), None), P(("rows", "feat"), None), P()),
        out_specs=(P(("rows", "feat")), P(("rows", "feat"), None)),
        check_vma=False,
    )
```

profile of v0, /device:TPU:0, one launch (start us, length us, event | category | flops | bytes accessed | tf_op | source)
XLA Modules:
  0.0 177.3 jit_solution(1144586767254924828)
XLA Ops:
  0.6 0.8 copy.40
  1.4 2.0 %all_gather.6 = bf16[64,128]{0,1:T(8,128)(2,1)S(1)} all-gather(bf16[64,64]{0,1:T(8,128)(2,1)S(1)} %copy.40), channel_id=1, replica_groups=mesh['rows'=16,'feat'=2] {'feat'}, dimensions={1}, use_global_device_ids=true | all-gather | bytes 24576 | tf_op jit(solution)/shard_map/all_gather | solution.py:16
  3.4 0.1 copy.41
  3.5 43.7 %all_gather.7 = bf16[1024,128]{1,0:T(8,128)(2,1)S(1)} all-gather(bf16[64,128]{1,0:T(8,128)(2,1)S(1)} %copy.41), channel_id=1, replica_groups=mesh['rows'=16,'feat'=2] {'rows'}, dimensions={0}, use_global_device_ids=true | all-gather | bytes 278528 | tf_op jit(solution)/shard_map/all_gather | solution.py:17
  47.2 0.7 convert_multiply_fusion.1
  47.9 18.8 %while.11 = (s32[]{:T(128)}, f32[1024]{0:T(1024)S(1)}, bf16[8,2048,128]{2,1,0:T(8,128)(2,1)}, bf16[1024,128]{1,0:T(8,128)(2,1)S(1)}, f32[1024]{0:T(1024)S(1)}, /*index=5*/s32[]{:T(128)}, s32[]{:T(128)}) while((s32[]{:T(128)}, f32[1024]{0:T(1024)S(1)}, bf16[8,2048,128]{2,1,0:T(8,128)(2,1)}, bf16[1024,128]{1,0:T(8,128)(2,1)S(1)}, ...), condition=%wide.region_2.3_spmd.clone, body=%wide.region_0.2_spmd.clone.sunk | while | flops 543163392 | bytes 807511 | solution.py:28
  47.9 2.3 %maximum_reduce_fusion.2 = f32[1024]{0:T(1024)S(1)} fusion(bf16[1024,128]{1,0:T(8,128)(2,1)S(1)} %get-tuple-element.115, f32[1024]{0:T(1024)S(1)} %get-tuple-element.116, bf16[8,2048,128]{2,1,0:T(8,128)(2,1)} %get-tuple-element.114, s32[]{:T(128)} %get-tuple-element.105), kind=kOutput, calls=%fused_computation.4.clone.1 | convolution fusion | flops 543161344 | bytes 795136 | tf_op jit(solution)/shard_map/while/body/eval_jaxpr/dot_general | solution.py:23
  50.2 2.3 %maximum_reduce_fusion.2 = f32[1024]{0:T(1024)S(1)} fusion(bf16[1024,128]{1,0:T(8,128)(2,1)S(1)} %get-tuple-element.115, f32[1024]{0:T(1024)S(1)} %get-tuple-element.116, bf16[8,2048,128]{2,1,0:T(8,128)(2,1)} %get-tuple-element.114, s32[]{:T(128)} %get-tuple-element.105), kind=kOutput, calls=%fused_computation.4.clone.1 | convolution fusion | flops 543161344 | bytes 795136 | tf_op jit(solution)/shard_map/while/body/eval_jaxpr/dot_general | solution.py:23
  52.6 2.3 %maximum_reduce_fusion.2 = f32[1024]{0:T(1024)S(1)} fusion(bf16[1024,128]{1,0:T(8,128)(2,1)S(1)} %get-tuple-element.115, f32[1024]{0:T(1024)S(1)} %get-tuple-element.116, bf16[8,2048,128]{2,1,0:T(8,128)(2,1)} %get-tuple-element.114, s32[]{:T(128)} %get-tuple-element.105), kind=kOutput, calls=%fused_computation.4.clone.1 | convolution fusion | flops 543161344 | bytes 795136 | tf_op jit(solution)/shard_map/while/body/eval_jaxpr/dot_general | solution.py:23
  54.9 2.3 %maximum_reduce_fusion.2 = f32[1024]{0:T(1024)S(1)} fusion(bf16[1024,128]{1,0:T(8,128)(2,1)S(1)} %get-tuple-element.115, f32[1024]{0:T(1024)S(1)} %get-tuple-element.116, bf16[8,2048,128]{2,1,0:T(8,128)(2,1)} %get-tuple-element.114, s32[]{:T(128)} %get-tuple-element.105), kind=kOutput, calls=%fused_computation.4.clone.1 | convolution fusion | flops 543161344 | bytes 795136 | tf_op jit(solution)/shard_map/while/body/eval_jaxpr/dot_general | solution.py:23
  57.3 2.3 %maximum_reduce_fusion.2 = f32[1024]{0:T(1024)S(1)} fusion(bf16[1024,128]{1,0:T(8,128)(2,1)S(1)} %get-tuple-element.115, f32[1024]{0:T(1024)S(1)} %get-tuple-element.116, bf16[8,2048,128]{2,1,0:T(8,128)(2,1)} %get-tuple-element.114, s32[]{:T(128)} %get-tuple-element.105), kind=kOutput, calls=%fused_computation.4.clone.1 | convolution fusion | flops 543161344 | bytes 795136 | tf_op jit(solution)/shard_map/while/body/eval_jaxpr/dot_general | solution.py:23
  59.6 2.3 %maximum_reduce_fusion.2 = f32[1024]{0:T(1024)S(1)} fusion(bf16[1024,128]{1,0:T(8,128)(2,1)S(1)} %get-tuple-element.115, f32[1024]{0:T(1024)S(1)} %get-tuple-element.116, bf16[8,2048,128]{2,1,0:T(8,128)(2,1)} %get-tuple-element.114, s32[]{:T(128)} %get-tuple-element.105), kind=kOutput, calls=%fused_computation.4.clone.1 | convolution fusion | flops 543161344 | bytes 795136 | tf_op jit(solution)/shard_map/while/body/eval_jaxpr/dot_general | solution.py:23
  62.0 2.3 %maximum_reduce_fusion.2 = f32[1024]{0:T(1024)S(1)} fusion(bf16[1024,128]{1,0:T(8,128)(2,1)S(1)} %get-tuple-element.115, f32[1024]{0:T(1024)S(1)} %get-tuple-element.116, bf16[8,2048,128]{2,1,0:T(8,128)(2,1)} %get-tuple-element.114, s32[]{:T(128)} %get-tuple-element.105), kind=kOutput, calls=%fused_computation.4.clone.1 | convolution fusion | flops 543161344 | bytes 795136 | tf_op jit(solution)/shard_map/while/body/eval_jaxpr/dot_general | solution.py:23
  64.3 2.3 %maximum_reduce_fusion.2 = f32[1024]{0:T(1024)S(1)} fusion(bf16[1024,128]{1,0:T(8,128)(2,1)S(1)} %get-tuple-element.115, f32[1024]{0:T(1024)S(1)} %get-tuple-element.116, bf16[8,2048,128]{2,1,0:T(8,128)(2,1)} %get-tuple-element.114, s32[]{:T(128)} %get-tuple-element.105), kind=kOutput, calls=%fused_computation.4.clone.1 | convolution fusion | flops 543161344 | bytes 795136 | tf_op jit(solution)/shard_map/while/body/eval_jaxpr/dot_general | solution.py:23
  66.7 0.7 reshape.217
  67.3 4.1 %all-to-all-start = ((f32[16,2,32]{2,1,0:T(2,128)}), f32[16,2,32]{2,1,0:T(2,128)}, u32[]{:S(2)}, u32[]{:S(2)}) async-start(f32[16,2,32]{2,1,0:T(2,128)} %reshape.217), calls=%async_computation | async-start | bytes 32768 | tf_op jit(solution)/shard_map/all_to_all | solution.py:70
  71.5 0.0 copy-done
  71.5 0.1 reshape.220
  71.6 0.1 reshape.219
  71.7 0.1 reshape.218
  71.8 0.1 fusion.6
  71.9 0.0 copy-start.2
  71.9 0.0 copy-start.1
  71.9 9.2 %reduce-window.6 = s32[32,25,128]{2,1,0:T(8,128)S(1)} reduce-window(s32[32,25,128]{2,1,0:T(8,128)S(1)} %fusion.6, s32[]{:T(128)} %constant.28.clone.1), window={size=1x1x128 pad=0_0x0_0x127_0}, to_apply=%region_4.5 | reduce-window | flops 13004800 | bytes 819204 | tf_op jit(solution)/shard_map/reduce-window
  81.1 0.8 slice_reduce_fusion
  81.9 0.2 reduce-window.9
  82.1 0.2 broadcast_add_fusion
  82.3 0.3 fusion.9
  82.6 0.1 or_reduce_fusion
  82.9 0.0 copy-done.2
  82.9 0.1 and_reduce_fusion
  83.0 0.1 pad_add_fusion.1
  83.1 0.6 broadcast_select_fusion
  83.7 0.5 copy.44
  84.2 13.8 %scatter_custom_fusion = s32[3200,2]{1,0:T(8,128)S(1)} fusion(s32[3200]{0:T(1024)} %broadcast_select_fusion, s32[3200,2]{1,0:T(8,128)S(1)} %copy.44, s32[]{:T(128)} %constant.28.clone.1), kind=kCustom, calls=%fused_computation.11 | custom fusion | bytes 26112
  98.1 1.3 reshape.222
  99.4 0.0 all-to-all-done
  99.4 0.7 copy.66
  100.1 0.1 reshape.269
  100.2 3.7 %all_to_all.30 = f32[2,1,512]{2,1,0:T(1,128)S(1)} all-to-all(f32[2,1,512]{2,1,0:T(1,128)S(1)} %reshape.269), channel_id=1, replica_groups=mesh['rows'=16,'feat'=2] {'feat'}, dimensions={0} | all-to-all | bytes 8192 | tf_op jit(solution)/shard_map/all_to_all | solution.py:69
  103.8 6.8 %all-to-all-start.2 = ((s32[16,2,200]{2,1,0:T(2,128)}), s32[16,2,200]{2,1,0:T(2,128)S(1)}, u32[]{:S(2)}, u32[]{:S(2)}) async-start(s32[16,2,200]{2,1,0:T(2,128)} %reshape.222), calls=%async_computation.2 | async-start | bytes 65536 | tf_op jit(solution)/shard_map/all_to_all | solution.py:42
  110.7 0.5 broadcast.292
  111.2 0.7 reduce.15
  111.8 0.1 reshape.270
  111.9 0.5 bitcast_reduce_fusion
  112.5 5.6 %all-to-all-done.2 = s32[16,2,200]{2,1,0:T(2,128)S(1)} async-done(((s32[16,2,200]{2,1,0:T(2,128)}), s32[16,2,200]{2,1,0:T(2,128)S(1)}, u32[]{:S(2)}, u32[]{:S(2)}) %all-to-all-start.2) | async-done | bytes 25632 | tf_op jit(solution)/shard_map/all_to_all | solution.py:42
  118.1 3.7 %all_to_all.31 = s32[16,2,200]{2,0,1:T(8,128)S(1)} all-to-all(s32[16,2,200]{2,0,1:T(8,128)S(1)} %copy.45), channel_id=1, replica_groups=mesh['rows'=16,'feat'=2] {'feat'}, dimensions={1} | all-to-all | bytes 51200 | tf_op jit(solution)/shard_map/all_to_all | solution.py:41
  121.8 0.5 reshape.223
  122.3 1.7 fusion.17
  124.0 1.9 %copy.57 = s32[3200,1]{0,1:T(1,128)S(1)} copy(s32[3200,1]{1,0:T(8,128)} %get-tuple-element.61) | data formatting | bytes 25600
  126.0 0.1 fusion.15
  126.0 6.7 %gather_fusion.1 = bf16[3200,128]{1,0:T(8,128)(2,1)S(1)} fusion(bf16[1024,128]{1,0:T(8,128)(2,1)S(1)} %get-tuple-element.119, s32[4096]{0:T(1024)S(1)} %pad_clamp_fusion), kind=kCustom, calls=%fused_computation.1 | custom fusion | bytes 1651200 | tf_op jit(solution)/shard_map/gather | solution.py:56
  132.8 0.5 copy.56
  133.3 0.1 fusion.14
  133.3 8.5 %gather_fusion = bf16[3200,128]{1,0:T(8,128)(2,1)S(1)} fusion(bf16[16384,128]{1,0:T(8,128)(2,1)} %bitcast.35, s32[4096]{0:T(1024)S(1)} %pad_clamp_fusion.1), kind=kCustom, calls=%fused_computation | custom fusion | bytes 1651200 | tf_op jit(solution)/shard_map/gather | solution.py:55
  141.8 0.0 copy-start.3
  141.9 0.5 fusion.3
  142.4 0.7 reshape.224
  143.1 3.5 %all-to-all-start.4 = ((f32[16,2,100]{2,1,0:T(2,128)}), f32[16,2,100]{2,1,0:T(2,128)S(1)}, u32[]{:S(2)}, u32[]{:S(2)}) async-start(f32[16,2,100]{2,1,0:T(2,128)} %reshape.224), calls=%async_computation.4 | async-start | bytes 32768 | tf_op jit(solution)/shard_map/all_to_all | solution.py:63
  146.6 0.5 broadcast_multiply_fusion
  147.1 6.8 %all-to-all-done.4 = f32[16,2,100]{2,1,0:T(2,128)S(1)} async-done(((f32[16,2,100]{2,1,0:T(2,128)}), f32[16,2,100]{2,1,0:T(2,128)S(1)}, u32[]{:S(2)}, u32[]{:S(2)}) %all-to-all-start.4) | async-done | bytes 12832 | tf_op jit(solution)/shard_map/all_to_all | solution.py:63
  153.9 3.7 %all_to_all.32 = f32[16,2,100]{2,0,1:T(8,128)S(1)} all-to-all(f32[16,2,100]{2,0,1:T(8,128)S(1)} %copy.49), channel_id=1, replica_groups=mesh['rows'=16,'feat'=2] {'feat'}, dimensions={1} | all-to-all | bytes 25600 | tf_op jit(solution)/shard_map/all_to_all | solution.py:62
  157.6 19.0 %gather_fusion.2 = f32[3200]{0:T(1024)S(1)} fusion(f32[32,100]{1,0:T(8,128)S(1)} %bitcast.33, s32[3200]{0:T(1024)S(1)} %get-tuple-element.58), kind=kCustom, calls=%fused_computation.2 | custom fusion | bytes 51200 | tf_op jit(solution)/shard_map/gather | solution.py:78
  176.6 0.7 reshape.226
  (22 shorter events, 0.2 us)
Async XLA Ops:
  47.9 23.6 %copy-start = (s32[32,100]{1,0:T(8,128)S(1)}, s32[32,100]{1,0:T(8,128)}, u32[]{:S(2)}) copy-start(s32[32,100]{1,0:T(8,128)} %param.8) | copy-start | bytes 38404
  67.3 32.0 %all-to-all-start = ((f32[16,2,32]{2,1,0:T(2,128)}), f32[16,2,32]{2,1,0:T(2,128)}, u32[]{:S(2)}, u32[]{:S(2)}) async-start(f32[16,2,32]{2,1,0:T(2,128)} %reshape.217), calls=%async_computation | async-start | bytes 32768 | tf_op jit(solution)/shard_map/all_to_all | solution.py:70
  71.9 11.0 %copy-start.2 = (s32[2]{0:T(128)S(1)}, s32[2]{0:T(128)}, u32[]{:S(2)}) copy-start(s32[2]{0:T(128)} %constant.67) | copy-start | bytes 28
  71.9 11.1 %copy-start.1 = (s32[2]{0:T(128)S(1)}, s32[2]{0:T(128)}, u32[]{:S(2)}) copy-start(s32[2]{0:T(128)} %constant.64) | copy-start | bytes 28
  103.8 14.2 %all-to-all-start.2 = ((s32[16,2,200]{2,1,0:T(2,128)}), s32[16,2,200]{2,1,0:T(2,128)S(1)}, u32[]{:S(2)}, u32[]{:S(2)}) async-start(s32[16,2,200]{2,1,0:T(2,128)} %reshape.222), calls=%async_computation.2 | async-start | bytes 65536 | tf_op jit(solution)/shard_map/all_to_all | solution.py:42
  141.8 4.8 %copy-start.3 = (f32[32]{0:T(128)S(1)}, f32[32]{0:T(128)}, u32[]{:S(2)}) copy-start(f32[32]{0:T(128)} %bitcast_reduce_fusion) | copy-start | bytes 388
  143.1 10.8 %all-to-all-start.4 = ((f32[16,2,100]{2,1,0:T(2,128)}), f32[16,2,100]{2,1,0:T(2,128)S(1)}, u32[]{:S(2)}, u32[]{:S(2)}) async-start(f32[16,2,100]{2,1,0:T(2,128)} %reshape.224), calls=%async_computation.4 | async-start | bytes 32768 | tf_op jit(solution)/shard_map/all_to_all | solution.py:63
where the time goes:
time: 178 us; the launch traced here: 177 us
  local copies, waits for them, and re-layouts  59.9 us (34%)
  blocking collectives  56.8 us (32%)
  matrix products  18.5 us (10%)
  starting transfers between devices  14.4 us (8%)
  other arithmetic  14.1 us (8%)
  waiting for transfers between devices  12.4 us (7%)
    all_gather x1, blocking collectives, body(): whole = lax.all_gather(full_rows, 'rows', axis=0, tiled=True)  43.7 us
    gather x1, local copies, waits for them, and re-layouts, body(): answers.reshape(shards, capacity)[target, rank]  19 us
    dot_general x8, matrix products, visit(): lax.dot_general(whole, block_rows, (((1,), (1,)), ((), ())), preferred_el...  18.5 us
    unnamed x14, local copies, waits for them, and re-layouts  17.2 us
    another operation x3, other arithmetic  9.61 us
    gather x1, local copies, waits for them, and re-layouts, body(): picked = corpus[received[:, 0]]  8.49 us
    all_to_all x1, starting transfers between devices, body(): lax.all_to_all(send_both.reshape(n_rows, n_feat, capacity * 2), 'rows', s...  6.81 us
    all_to_all x1, waiting for transfers between devices, body(): lax.all_to_all(values, 'rows', split_axis=0, concat_axis=0, tiled=True)  6.78 us
  transfers between devices with their start and end apart: 3, of which 2 were waited for; matrix products, arithmetic and copies ran while one was open for 17% of the time, Pallas kernels for 0%

commit v1 on v0

--- a/solution.py
+++ b/solution.py
@@ -2,6 +2,29 @@
 import jax.numpy as jnp
 from jax import lax
 from jax.sharding import PartitionSpec as P
+
+
+def meet_signs_all(here_x, axis_tag="rows"):
+    g_now, small, high = (
+        lax.psum(1, axis_name=axis_tag),
+        lax.axis_index(axis_tag),
+        here_x.shape[0],
+    )
+    grid = [(idx, (idx + 1) % g_now) for idx in range(g_now)]
+    stack_in = [(idx, (idx - 1) % g_now) for idx in range(g_now)]
+    y1 = jnp.zeros((*here_x.shape[:0], g_now * high, *here_x.shape[1:]), here_x.dtype)
+    y1 = lax.dynamic_update_slice_in_dim(y1, here_x, small * high, axis=0)
+    y = response = here_x
+    known = g_now // 2
+    b = 1
+    while b < known + 1:
+        y = lax.ppermute(y, axis_name=axis_tag, perm=grid)
+        y1 = lax.dynamic_update_slice_in_dim(y1, y, (small - b) % g_now * high, axis=0)
+        if b < g_now - known:
+            response = lax.ppermute(response, perm=stack_in, axis_name=axis_tag)
+            y1 = lax.dynamic_update_slice_in_dim(y1, response, (small + b) % g_now * high, axis=0)
+        b = b + 1
+    return y1
 
 
 def body(queries, corpus, candidates, threshold):
@@ -14,7 +37,7 @@
     cutoff = threshold.astype(jnp.float32) * 0.01
     owner = lax.axis_index(("rows", "feat"))
     full_rows = lax.all_gather(queries, "feat", axis=1, tiled=True)
-    whole = lax.all_gather(full_rows, "rows", axis=0, tiled=True)
+    whole = meet_signs_all(full_rows)
     query_count = whole.shape[0]
     block = 2048
     corpus_blocks = corpus.reshape(rows_dev // block, block, width)

time: 178 us -> 190 us (1.067)
  blocking collectives: 56.8 us -> 13.1 us
  starting transfers between devices: 14.4 us -> 51.1 us
  waiting for transfers between devices: 12.4 us -> 25 us
  local copies, waits for them, and re-layouts: 59.9 us -> 67 us
    all_gather x1 -> x0, blocking collectives: 43.7 us -> none  [body(): whole = lax.all_gather(full_rows, 'rows', axis=0, tiled=True)]
    ppermute x0 -> x15, starting transfers between devices: none -> 40.6 us  [the longest x7 35.9 us: meet_signs_all(): response = lax.ppermute(response, perm=stack_in, axis_name=axis_tag)]
    ppermute x0 -> x15, waiting for transfers between devices: none -> 13.4 us  [the longest x8 13.4 us: meet_signs_all(): y = lax.ppermute(y, axis_name=axis_tag, perm=grid)]
    all_to_all x1, waiting for transfers between devices: 0.01 us -> 6.08 us  [body(): lax.all_to_all(partials, 'rows', split_axis=0, concat_axis=0, tiled=True)]
    all_to_all x1, waiting for transfers between devices: 5.6 us -> 0.01 us  [body(): lax.all_to_all(send_both.reshape(n_rows, n_feat, capacity * 2), 'rows', s...]
    dynamic_update_slice x0 -> x16, local copies, waits for them, and re-layouts: none -> 5.15 us  [the longest x8 2.21 us: meet_signs_all(): lax.dynamic_update_slice_in_dim(y1, y, (small - b) % g_now * high, axis=0)]
    all_to_all x1, starting transfers between devices: 6.81 us -> 3.5 us  [body(): lax.all_to_all(send_both.reshape(n_rows, n_feat, capacity * 2), 'rows', s...]
    reshape x3, local copies, waits for them, and re-layouts: 0.31 us -> 2.46 us  [body(): flat_ids = candidates.reshape(-1)]
  transfers between devices with their start and end apart: 3 -> 18, of which waited for: 2 -> 8; matrix products, arithmetic and copies ran while one was open for 17% -> 27% of each run, Pallas kernels for 0% -> 0%
where the time goes in v1:
time: 190 us; the launch traced here: 189 us
  local copies, waits for them, and re-layouts  67 us (35%)
  starting transfers between devices  51.1 us (27%)
  waiting for transfers between devices  25 us (13%)
  matrix products  18.4 us (10%)
  blocking collectives  13.1 us (7%)
  other arithmetic  12.9 us (7%)
    ppermute x7, starting transfers between devices, meet_signs_all(): response = lax.ppermute(response, perm=stack_in, axis_name=axis_tag)  35.9 us
    gather x1, local copies, waits for them, and re-layouts, body(): answers.reshape(shards, capacity)[target, rank]  19 us
    dot_general x8, matrix products, visit(): lax.dot_general(whole, block_rows, (((1,), (1,)), ((), ())), preferred_el...  18.4 us
    unnamed x16, local copies, waits for them, and re-layouts  17.1 us
    ppermute x8, waiting for transfers between devices, meet_signs_all(): y = lax.ppermute(y, axis_name=axis_tag, perm=grid)  13.4 us
    another operation x3, other arithmetic  9.61 us
    gather x1, local copies, waits for them, and re-layouts, body(): picked = corpus[received[:, 0]]  8.49 us
    gather x1, local copies, waits for them, and re-layouts, body(): asked = whole[received[:, 1]]  6.72 us
  transfers between devices with their start and end apart: 18, of which 8 were waited for; matrix products, arithmetic and copies ran while one was open for 27% of the time, Pallas kernels for 0%

profile of v1, /device:TPU:0, one launch (start us, length us, event | category | flops | bytes accessed | tf_op | source)
XLA Modules:
  0.0 188.9 jit_solution(9508828512468099624)
XLA Ops:
  0.6 0.8 copy.44
  1.4 2.0 %all_gather.3 = bf16[64,128]{0,1:T(8,128)(2,1)S(1)} all-gather(bf16[64,64]{0,1:T(8,128)(2,1)S(1)} %copy.44), channel_id=1, replica_groups=mesh['rows'=16,'feat'=2] {'feat'}, dimensions={1}, use_global_device_ids=true | all-gather | bytes 24576 | tf_op jit(solution)/shard_map/all_gather | solution.py:39
  3.4 0.7 copy.45
  4.1 2.8 %collective-permute-start = (bf16[64,128]{1,0:T(8,128)(2,1)}, bf16[64,128]{1,0:T(8,128)(2,1)}, u32[]{:S(2)}, u32[]{:S(2)}) collective-permute-start(bf16[64,128]{1,0:T(8,128)(2,1)} %copy.45), channel_id=1, source_target_pairs={{0,2},{2,4},{4,6},{6,8},{8,10},{10,12},{12,14},{14,16},{16,18},{18... | collective-permute-start | bytes 49160 | tf_op jit(solution)/shard_map/ppermute | solution.py:21
  6.9 4.0 %collective-permute-start.1 = (bf16[64,128]{1,0:T(8,128)(2,1)}, bf16[64,128]{1,0:T(8,128)(2,1)}, u32[]{:S(2)}, u32[]{:S(2)}) collective-permute-start(bf16[64,128]{1,0:T(8,128)(2,1)} %copy.45), channel_id=1, source_target_pairs={{0,30},{2,0},{4,2},{6,4},{8,6},{10,8},{12,10},{14,12},{16,14},{18,... | collective-permute-start | bytes 49160 | tf_op jit(solution)/shard_map/ppermute | solution.py:24
  10.9 0.8 reshape.220
  11.7 0.8 reshape.219
  12.6 0.8 reshape.218
  13.5 9.2 %reduce-window.6 = s32[32,25,128]{2,1,0:T(8,128)S(1)} reduce-window(s32[32,25,128]{2,1,0:T(8,128)S(1)} %fusion.6, s32[]{:T(128)} %constant.133.clone.1), window={size=1x1x128 pad=0_0x0_0x127_0}, to_apply=%region_4.5 | reduce-window | flops 13004800 | bytes 819204 | tf_op jit(solution)/shard_map/reduce-window
  22.8 0.8 slice_reduce_fusion
  24.7 0.5 copy.50
  25.3 13.7 %scatter_custom_fusion = s32[3200,2]{1,0:T(8,128)S(1)} fusion(s32[3200]{0:T(1024)S(1)} %broadcast_select_fusion, s32[3200,2]{1,0:T(8,128)S(1)} %copy.50, s32[]{:T(128)} %constant.133.clone.1), kind=kCustom, calls=%fused_computation.11 | custom fusion | bytes 25604
  39.0 1.3 reshape.222
  40.3 3.5 %all-to-all-start.2 = ((s32[16,2,200]{2,1,0:T(2,128)}), s32[16,2,200]{2,1,0:T(2,128)S(1)}, u32[]{:S(2)}, u32[]{:S(2)}) async-start(s32[16,2,200]{2,1,0:T(2,128)} %reshape.222), calls=%async_computation.2 | async-start | bytes 65536 | tf_op jit(solution)/shard_map/all_to_all | solution.py:65
  43.8 0.6 convert_multiply_fusion.1
  44.4 0.7 constant_dynamic-update-slice_fusion.15
  45.1 1.8 collective-permute-start.2
  47.0 3.8 %collective-permute-start.3 = (bf16[64,128]{1,0:T(8,128)(2,1)}, bf16[64,128]{1,0:T(8,128)(2,1)}, u32[]{:S(2)}, u32[]{:S(2)}) collective-permute-start(bf16[64,128]{1,0:T(8,128)(2,1)} %collective-permute-done.1), channel_id=1, source_target_pairs={{0,30},{2,0},{4,2},{6,4},{8,6},{10,8},{12,10},{14,12},{16,14},{18,... | collective-permute-start | bytes 49160 | tf_op jit(solution)/shard_map/ppermute | solution.py:24
  50.8 0.7 constant_dynamic-update-slice_fusion.14
  51.5 0.7 constant_dynamic-update-slice_fusion.13
  52.2 0.6 collective-permute-done.2
  52.8 5.6 %collective-permute-start.5 = (bf16[64,128]{1,0:T(8,128)(2,1)}, bf16[64,128]{1,0:T(8,128)(2,1)}, u32[]{:S(2)}, u32[]{:S(2)}) collective-permute-start(bf16[64,128]{1,0:T(8,128)(2,1)} %collective-permute-done.3), channel_id=1, source_target_pairs={{0,30},{2,0},{4,2},{6,4},{8,6},{10,8},{12,10},{14,12},{16,14},{18,... | collective-permute-start | bytes 49160 | tf_op jit(solution)/shard_map/ppermute | solution.py:24
  58.4 0.7 constant_dynamic-update-slice_fusion.12
  59.1 0.7 constant_dynamic-update-slice_fusion.11
  59.9 3.7 %all_to_all.30 = s32[16,2,200]{2,0,1:T(8,128)S(1)} all-to-all(s32[16,2,200]{2,0,1:T(8,128)S(1)} %copy.51), channel_id=1, replica_groups=mesh['rows'=16,'feat'=2] {'feat'}, dimensions={1} | all-to-all | bytes 51200 | tf_op jit(solution)/shard_map/all_to_all | solution.py:64
  63.6 0.5 reshape.223
  64.2 1.7 fusion.17
  65.9 1.9 %copy.63 = s32[3200,1]{0,1:T(1,128)S(1)} copy(s32[3200,1]{1,0:T(8,128)} %get-tuple-element.61) | data formatting | bytes 25600
  67.9 0.5 copy.62
  68.4 8.5 %gather_fusion = bf16[3200,128]{1,0:T(8,128)(2,1)S(1)} fusion(bf16[16384,128]{1,0:T(8,128)(2,1)} %param.7, s32[4096]{0:T(1024)S(1)} %pad_clamp_fusion.1), kind=kCustom, calls=%fused_computation | custom fusion | bytes 1651200 | tf_op jit(solution)/shard_map/gather | solution.py:78
  77.0 5.6 %collective-permute-start.7 = (bf16[64,128]{1,0:T(8,128)(2,1)}, bf16[64,128]{1,0:T(8,128)(2,1)S(1)}, u32[]{:S(2)}, u32[]{:S(2)}) collective-permute-start(bf16[64,128]{1,0:T(8,128)(2,1)} %collective-permute-done.5), channel_id=1, source_target_pairs={{0,30},{2,0},{4,2},{6,4},{8,6},{10,8},{12,10},{14,12},{16,14},{18,... | collective-permute-start | bytes 49160 | tf_op jit(solution)/shard_map/ppermute | solution.py:24
  82.6 0.7 constant_dynamic-update-slice_fusion.10
  83.3 0.7 constant_dynamic-update-slice_fusion.9
  84.5 5.6 %collective-permute-start.9 = (bf16[64,128]{1,0:T(8,128)(2,1)S(1)}, bf16[64,128]{1,0:T(8,128)(2,1)S(1)}, u32[]{:S(2)}, u32[]{:S(2)}) collective-permute-start(bf16[64,128]{1,0:T(8,128)(2,1)S(1)} %collective-permute-done.7), channel_id=1, source_target_pairs={{0,30},{2,0},{4,2},{6,4},{8,6},{10,8},{12,10},{14,12},{16,14},{18,... | collective-permute-start | bytes 49160 | tf_op jit(solution)/shard_map/ppermute | solution.py:24
  90.2 1.7 collective-permute-done.8
  91.9 5.6 %collective-permute-start.11 = (bf16[64,128]{1,0:T(8,128)(2,1)S(1)}, bf16[64,128]{1,0:T(8,128)(2,1)S(1)}, u32[]{:S(2)}, u32[]{:S(2)}) collective-permute-start(bf16[64,128]{1,0:T(8,128)(2,1)S(1)} %collective-permute-done.9), channel_id=1, source_target_pairs={{0,30},{2,0},{4,2},{6,4},{8,6},{10,8},{12,10},{14,12},{16,14},{18,... | collective-permute-start | bytes 49160 | tf_op jit(solution)/shard_map/ppermute | solution.py:24
  97.5 1.7 collective-permute-done.10
  99.2 5.6 %collective-permute-start.13 = (bf16[64,128]{1,0:T(8,128)(2,1)S(1)}, bf16[64,128]{1,0:T(8,128)(2,1)S(1)}, u32[]{:S(2)}, u32[]{:S(2)}) collective-permute-start(bf16[64,128]{1,0:T(8,128)(2,1)S(1)} %collective-permute-done.11), channel_id=1, source_target_pairs={{0,30},{2,0},{4,2},{6,4},{8,6},{10,8},{12,10},{14,12},{16,14},{18,... | collective-permute-start | bytes 49160 | tf_op jit(solution)/shard_map/ppermute | solution.py:24
  104.8 1.7 collective-permute-done.12
  106.6 7.3 %collective-permute-done.14 = bf16[64,128]{1,0:T(8,128)(2,1)S(1)} collective-permute-done((bf16[64,128]{1,0:T(8,128)(2,1)S(1)}, bf16[64,128]{1,0:T(8,128)(2,1)S(1)}, u32[]{:S(2)}, u32[]{:S(2)}) %collective-permute-start.14) | collective-permute-done | bytes 16416 | tf_op jit(solution)/shard_map/ppermute | solution.py:21
  113.9 6.7 %gather_fusion.1 = bf16[3200,128]{1,0:T(8,128)(2,1)S(1)} fusion(bf16[1024,128]{1,0:T(8,128)(2,1)S(1)} %constant_dynamic-update-slice_fusion, s32[4096]{0:T(1024)S(1)} %pad_clamp_fusion), kind=kCustom, calls=%fused_computation.1 | custom fusion | bytes 1651200 | tf_op jit(solution)/shard_map/gather | solution.py:79
  120.6 18.8 %while.11 = (s32[]{:T(128)}, f32[1024]{0:T(1024)S(1)}, bf16[8,2048,128]{2,1,0:T(8,128)(2,1)}, bf16[1024,128]{1,0:T(8,128)(2,1)S(1)}, f32[1024]{0:T(1024)S(1)}, /*index=5*/s32[]{:T(128)}, s32[]{:T(128)}) while((s32[]{:T(128)}, f32[1024]{0:T(1024)S(1)}, bf16[8,2048,128]{2,1,0:T(8,128)(2,1)}, bf16[1024,128]{1,0:T(8,128)(2,1)S(1)}, ...), condition=%wide.region_2.3_spmd.clone, body=%wide.region_0.2_spmd.clone.sunk | while | flops 543163392 | bytes 807511 | solution.py:51
  120.6 2.3 %maximum_reduce_fusion.2 = f32[1024]{0:T(1024)S(1)} fusion(bf16[1024,128]{1,0:T(8,128)(2,1)S(1)} %get-tuple-element.115, f32[1024]{0:T(1024)S(1)} %get-tuple-element.116, bf16[8,2048,128]{2,1,0:T(8,128)(2,1)} %get-tuple-element.114, s32[]{:T(128)} %get-tuple-element.105), kind=kOutput, calls=%fused_computation.4.clone.1 | convolution fusion | flops 543161344 | bytes 795136 | tf_op jit(solution)/shard_map/while/body/eval_jaxpr/dot_general | solution.py:46
  123.0 2.3 %maximum_reduce_fusion.2 = f32[1024]{0:T(1024)S(1)} fusion(bf16[1024,128]{1,0:T(8,128)(2,1)S(1)} %get-tuple-element.115, f32[1024]{0:T(1024)S(1)} %get-tuple-element.116, bf16[8,2048,128]{2,1,0:T(8,128)(2,1)} %get-tuple-element.114, s32[]{:T(128)} %get-tuple-element.105), kind=kOutput, calls=%fused_computation.4.clone.1 | convolution fusion | flops 543161344 | bytes 795136 | tf_op jit(solution)/shard_map/while/body/eval_jaxpr/dot_general | solution.py:46
  125.3 2.3 %maximum_reduce_fusion.2 = f32[1024]{0:T(1024)S(1)} fusion(bf16[1024,128]{1,0:T(8,128)(2,1)S(1)} %get-tuple-element.115, f32[1024]{0:T(1024)S(1)} %get-tuple-element.116, bf16[8,2048,128]{2,1,0:T(8,128)(2,1)} %get-tuple-element.114, s32[]{:T(128)} %get-tuple-element.105), kind=kOutput, calls=%fused_computation.4.clone.1 | convolution fusion | flops 543161344 | bytes 795136 | tf_op jit(solution)/shard_map/while/body/eval_jaxpr/dot_general | solution.py:46
  127.7 2.3 %maximum_reduce_fusion.2 = f32[1024]{0:T(1024)S(1)} fusion(bf16[1024,128]{1,0:T(8,128)(2,1)S(1)} %get-tuple-element.115, f32[1024]{0:T(1024)S(1)} %get-tuple-element.116, bf16[8,2048,128]{2,1,0:T(8,128)(2,1)} %get-tuple-element.114, s32[]{:T(128)} %get-tuple-element.105), kind=kOutput, calls=%fused_computation.4.clone.1 | convolution fusion | flops 543161344 | bytes 795136 | tf_op jit(solution)/shard_map/while/body/eval_jaxpr/dot_general | solution.py:46
  130.0 2.3 %maximum_reduce_fusion.2 = f32[1024]{0:T(1024)S(1)} fusion(bf16[1024,128]{1,0:T(8,128)(2,1)S(1)} %get-tuple-element.115, f32[1024]{0:T(1024)S(1)} %get-tuple-element.116, bf16[8,2048,128]{2,1,0:T(8,128)(2,1)} %get-tuple-element.114, s32[]{:T(128)} %get-tuple-element.105), kind=kOutput, calls=%fused_computation.4.clone.1 | convolution fusion | flops 543161344 | bytes 795136 | tf_op jit(solution)/shard_map/while/body/eval_jaxpr/dot_general | solution.py:46
  132.4 2.3 %maximum_reduce_fusion.2 = f32[1024]{0:T(1024)S(1)} fusion(bf16[1024,128]{1,0:T(8,128)(2,1)S(1)} %get-tuple-element.115, f32[1024]{0:T(1024)S(1)} %get-tuple-element.116, bf16[8,2048,128]{2,1,0:T(8,128)(2,1)} %get-tuple-element.114, s32[]{:T(128)} %get-tuple-element.105), kind=kOutput, calls=%fused_computation.4.clone.1 | convolution fusion | flops 543161344 | bytes 795136 | tf_op jit(solution)/shard_map/while/body/eval_jaxpr/dot_general | solution.py:46
  134.7 2.3 %maximum_reduce_fusion.2 = f32[1024]{0:T(1024)S(1)} fusion(bf16[1024,128]{1,0:T(8,128)(2,1)S(1)} %get-tuple-element.115, f32[1024]{0:T(1024)S(1)} %get-tuple-element.116, bf16[8,2048,128]{2,1,0:T(8,128)(2,1)} %get-tuple-element.114, s32[]{:T(128)} %get-tuple-element.105), kind=kOutput, calls=%fused_computation.4.clone.1 | convolution fusion | flops 543161344 | bytes 795136 | tf_op jit(solution)/shard_map/while/body/eval_jaxpr/dot_general | solution.py:46
  137.1 2.3 %maximum_reduce_fusion.2 = f32[1024]{0:T(1024)S(1)} fusion(bf16[1024,128]{1,0:T(8,128)(2,1)S(1)} %get-tuple-element.115, f32[1024]{0:T(1024)S(1)} %get-tuple-element.116, bf16[8,2048,128]{2,1,0:T(8,128)(2,1)} %get-tuple-element.114, s32[]{:T(128)} %get-tuple-element.105), kind=kOutput, calls=%fused_computation.4.clone.1 | convolution fusion | flops 543161344 | bytes 795136 | tf_op jit(solution)/shard_map/while/body/eval_jaxpr/dot_general | solution.py:46
  139.4 0.7 reshape.217
  140.1 3.5 %all-to-all-start = ((f32[16,2,32]{2,1,0:T(2,128)}), f32[16,2,32]{2,1,0:T(2,128)S(1)}, u32[]{:S(2)}, u32[]{:S(2)}) async-start(f32[16,2,32]{2,1,0:T(2,128)} %reshape.217), calls=%async_computation | async-start | bytes 32768 | tf_op jit(solution)/shard_map/all_to_all | solution.py:93
  143.6 0.5 fusion.3
  144.1 0.7 reshape.224
  144.8 6.1 %all-to-all-done = f32[16,2,32]{2,1,0:T(2,128)S(1)} async-done(((f32[16,2,32]{2,1,0:T(2,128)}), f32[16,2,32]{2,1,0:T(2,128)S(1)}, u32[]{:S(2)}, u32[]{:S(2)}) %all-to-all-start) | async-done | bytes 4128 | tf_op jit(solution)/shard_map/all_to_all | solution.py:93
  151.0 3.7 %all_to_all.31 = f32[2,1,512]{2,1,0:T(1,128)S(1)} all-to-all(f32[2,1,512]{2,1,0:T(1,128)S(1)} %reshape.269), channel_id=1, replica_groups=mesh['rows'=16,'feat'=2] {'feat'}, dimensions={0} | all-to-all | bytes 8192 | tf_op jit(solution)/shard_map/all_to_all | solution.py:92
  154.7 3.5 %all-to-all-start.4 = ((f32[16,2,100]{2,1,0:T(2,128)}), f32[16,2,100]{2,1,0:T(2,128)S(1)}, u32[]{:S(2)}, u32[]{:S(2)}) async-start(f32[16,2,100]{2,1,0:T(2,128)} %reshape.224), calls=%async_computation.4 | async-start | bytes 32768 | tf_op jit(solution)/shard_map/all_to_all | solution.py:86
  158.2 0.5 broadcast.322
  158.7 0.7 reduce.15
  159.5 0.5 broadcast_multiply_fusion
  160.0 5.5 %all-to-all-done.4 = f32[16,2,100]{2,1,0:T(2,128)S(1)} async-done(((f32[16,2,100]{2,1,0:T(2,128)}), f32[16,2,100]{2,1,0:T(2,128)S(1)}, u32[]{:S(2)}, u32[]{:S(2)}) %all-to-all-start.4) | async-done | bytes 12832 | tf_op jit(solution)/shard_map/all_to_all | solution.py:86
  165.5 3.7 %all_to_all.32 = f32[16,2,100]{2,0,1:T(8,128)S(1)} all-to-all(f32[16,2,100]{2,0,1:T(8,128)S(1)} %copy.55), channel_id=1, replica_groups=mesh['rows'=16,'feat'=2] {'feat'}, dimensions={1} | all-to-all | bytes 25600 | tf_op jit(solution)/shard_map/all_to_all | solution.py:85
  169.2 19.0 %gather_fusion.2 = f32[3200]{0:T(1024)S(1)} fusion(f32[32,100]{1,0:T(8,128)S(1)} %bitcast.33, s32[3200]{0:T(1024)S(1)} %get-tuple-element.58), kind=kCustom, calls=%fused_computation.2 | custom fusion | bytes 51200 | tf_op jit(solution)/shard_map/gather | solution.py:101
  188.2 0.7 reshape.226
  (70 shorter events, 2.3 us)
Async XLA Ops:
  4.1 41.0 %collective-permute-start = (bf16[64,128]{1,0:T(8,128)(2,1)}, bf16[64,128]{1,0:T(8,128)(2,1)}, u32[]{:S(2)}, u32[]{:S(2)}) collective-permute-start(bf16[64,128]{1,0:T(8,128)(2,1)} %copy.45), channel_id=1, source_target_pairs={{0,2},{2,4},{4,6},{6,8},{8,10},{10,12},{12,14},{14,16},{16,18},{18... | collective-permute-start | bytes 49160 | tf_op jit(solution)/shard_map/ppermute | solution.py:21
  6.9 40.0 %collective-permute-start.1 = (bf16[64,128]{1,0:T(8,128)(2,1)}, bf16[64,128]{1,0:T(8,128)(2,1)}, u32[]{:S(2)}, u32[]{:S(2)}) collective-permute-start(bf16[64,128]{1,0:T(8,128)(2,1)} %copy.45), channel_id=1, source_target_pairs={{0,30},{2,0},{4,2},{6,4},{8,6},{10,8},{12,10},{14,12},{16,14},{18,... | collective-permute-start | bytes 49160 | tf_op jit(solution)/shard_map/ppermute | solution.py:24
  13.5 11.0 %copy-start.4 = (s32[2]{0:T(128)S(1)}, s32[2]{0:T(128)}, u32[]{:S(2)}) copy-start(s32[2]{0:T(128)} %constant.167) | copy-start | bytes 28
  13.5 11.1 %copy-start.3 = (s32[2]{0:T(128)S(1)}, s32[2]{0:T(128)}, u32[]{:S(2)}) copy-start(s32[2]{0:T(128)} %constant.164) | copy-start | bytes 28
  25.3 18.5 %copy-start.1 = (s32[1024]{0:T(1024)S(1)}, s32[1024]{0:T(1024)}, u32[]{:S(2)}) copy-start(s32[1024]{0:T(1024)} %param.9) | copy-start | bytes 12292
  40.3 19.6 %all-to-all-start.2 = ((s32[16,2,200]{2,1,0:T(2,128)}), s32[16,2,200]{2,1,0:T(2,128)S(1)}, u32[]{:S(2)}, u32[]{:S(2)}) async-start(s32[16,2,200]{2,1,0:T(2,128)} %reshape.222), calls=%async_computation.2 | async-start | bytes 65536 | tf_op jit(solution)/shard_map/all_to_all | solution.py:65
  45.1 7.7 %collective-permute-start.2 = (bf16[64,128]{1,0:T(8,128)(2,1)}, bf16[64,128]{1,0:T(8,128)(2,1)}, u32[]{:S(2)}, u32[]{:S(2)}) collective-permute-start(bf16[64,128]{1,0:T(8,128)(2,1)} %collective-permute-done), channel_id=1, source_target_pairs={{0,2},{2,4},{4,6},{6,8},{8,10},{10,12},{12,14},{14,16},{16,18},{18... | collective-permute-start | bytes 49160 | tf_op jit(solution)/shard_map/ppermute | solution.py:21
  47.0 5.8 %collective-permute-start.3 = (bf16[64,128]{1,0:T(8,128)(2,1)}, bf16[64,128]{1,0:T(8,128)(2,1)}, u32[]{:S(2)}, u32[]{:S(2)}) collective-permute-start(bf16[64,128]{1,0:T(8,128)(2,1)} %collective-permute-done.1), channel_id=1, source_target_pairs={{0,30},{2,0},{4,2},{6,4},{8,6},{10,8},{12,10},{14,12},{16,14},{18,... | collective-permute-start | bytes 49160 | tf_op jit(solution)/shard_map/ppermute | solution.py:24
  52.8 24.1 %collective-permute-start.4 = (bf16[64,128]{1,0:T(8,128)(2,1)}, bf16[64,128]{1,0:T(8,128)(2,1)}, u32[]{:S(2)}, u32[]{:S(2)}) collective-permute-start(bf16[64,128]{1,0:T(8,128)(2,1)} %collective-permute-done.2), channel_id=1, source_target_pairs={{0,2},{2,4},{4,6},{6,8},{8,10},{10,12},{12,14},{14,16},{16,18},{18... | collective-permute-start | bytes 49160 | tf_op jit(solution)/shard_map/ppermute | solution.py:21
  52.8 24.2 %collective-permute-start.5 = (bf16[64,128]{1,0:T(8,128)(2,1)}, bf16[64,128]{1,0:T(8,128)(2,1)}, u32[]{:S(2)}, u32[]{:S(2)}) collective-permute-start(bf16[64,128]{1,0:T(8,128)(2,1)} %collective-permute-done.3), channel_id=1, source_target_pairs={{0,30},{2,0},{4,2},{6,4},{8,6},{10,8},{12,10},{14,12},{16,14},{18,... | collective-permute-start | bytes 49160 | tf_op jit(solution)/shard_map/ppermute | solution.py:24
  76.9 7.6 %collective-permute-start.6 = (bf16[64,128]{1,0:T(8,128)(2,1)}, bf16[64,128]{1,0:T(8,128)(2,1)S(1)}, u32[]{:S(2)}, u32[]{:S(2)}) collective-permute-start(bf16[64,128]{1,0:T(8,128)(2,1)} %collective-permute-done.4), channel_id=1, source_target_pairs={{0,2},{2,4},{4,6},{6,8},{8,10},{10,12},{12,14},{14,16},{16,18},{18... | collective-permute-start | bytes 49160 | tf_op jit(solution)/shard_map/ppermute | solution.py:21
  77.0 7.5 %collective-permute-start.7 = (bf16[64,128]{1,0:T(8,128)(2,1)}, bf16[64,128]{1,0:T(8,128)(2,1)S(1)}, u32[]{:S(2)}, u32[]{:S(2)}) collective-permute-start(bf16[64,128]{1,0:T(8,128)(2,1)} %collective-permute-done.5), channel_id=1, source_target_pairs={{0,30},{2,0},{4,2},{6,4},{8,6},{10,8},{12,10},{14,12},{16,14},{18,... | collective-permute-start | bytes 49160 | tf_op jit(solution)/shard_map/ppermute | solution.py:24
  84.5 7.3 %collective-permute-start.8 = (bf16[64,128]{1,0:T(8,128)(2,1)S(1)}, bf16[64,128]{1,0:T(8,128)(2,1)S(1)}, u32[]{:S(2)}, u32[]{:S(2)}) collective-permute-start(bf16[64,128]{1,0:T(8,128)(2,1)S(1)} %collective-permute-done.6), channel_id=1, source_target_pairs={{0,2},{2,4},{4,6},{6,8},{8,10},{10,12},{12,14},{14,16},{16,18},{18... | collective-permute-start | bytes 49160 | tf_op jit(solution)/shard_map/ppermute | solution.py:21
  84.5 7.3 %collective-permute-start.9 = (bf16[64,128]{1,0:T(8,128)(2,1)S(1)}, bf16[64,128]{1,0:T(8,128)(2,1)S(1)}, u32[]{:S(2)}, u32[]{:S(2)}) collective-permute-start(bf16[64,128]{1,0:T(8,128)(2,1)S(1)} %collective-permute-done.7), channel_id=1, source_target_pairs={{0,30},{2,0},{4,2},{6,4},{8,6},{10,8},{12,10},{14,12},{16,14},{18,... | collective-permute-start | bytes 49160 | tf_op jit(solution)/shard_map/ppermute | solution.py:24
  91.9 7.3 %collective-permute-start.10 = (bf16[64,128]{1,0:T(8,128)(2,1)S(1)}, bf16[64,128]{1,0:T(8,128)(2,1)S(1)}, u32[]{:S(2)}, u32[]{:S(2)}) collective-permute-start(bf16[64,128]{1,0:T(8,128)(2,1)S(1)} %collective-permute-done.8), channel_id=1, source_target_pairs={{0,2},{2,4},{4,6},{6,8},{8,10},{10,12},{12,14},{14,16},{16,18},{18... | collective-permute-start | bytes 49160 | tf_op jit(solution)/shard_map/ppermute | solution.py:21
  91.9 7.3 %collective-permute-start.11 = (bf16[64,128]{1,0:T(8,128)(2,1)S(1)}, bf16[64,128]{1,0:T(8,128)(2,1)S(1)}, u32[]{:S(2)}, u32[]{:S(2)}) collective-permute-start(bf16[64,128]{1,0:T(8,128)(2,1)S(1)} %collective-permute-done.9), channel_id=1, source_target_pairs={{0,30},{2,0},{4,2},{6,4},{8,6},{10,8},{12,10},{14,12},{16,14},{18,... | collective-permute-start | bytes 49160 | tf_op jit(solution)/shard_map/ppermute | solution.py:24
  99.2 7.3 %collective-permute-start.12 = (bf16[64,128]{1,0:T(8,128)(2,1)S(1)}, bf16[64,128]{1,0:T(8,128)(2,1)S(1)}, u32[]{:S(2)}, u32[]{:S(2)}) collective-permute-start(bf16[64,128]{1,0:T(8,128)(2,1)S(1)} %collective-permute-done.10), channel_id=1, source_target_pairs={{0,2},{2,4},{4,6},{6,8},{8,10},{10,12},{12,14},{14,16},{16,18},{18... | collective-permute-start | bytes 49160 | tf_op jit(solution)/shard_map/ppermute | solution.py:21
  99.2 7.3 %collective-permute-start.13 = (bf16[64,128]{1,0:T(8,128)(2,1)S(1)}, bf16[64,128]{1,0:T(8,128)(2,1)S(1)}, u32[]{:S(2)}, u32[]{:S(2)}) collective-permute-start(bf16[64,128]{1,0:T(8,128)(2,1)S(1)} %collective-permute-done.11), channel_id=1, source_target_pairs={{0,30},{2,0},{4,2},{6,4},{8,6},{10,8},{12,10},{14,12},{16,14},{18,... | collective-permute-start | bytes 49160 | tf_op jit(solution)/shard_map/ppermute | solution.py:24
  106.5 7.3 %collective-permute-start.14 = (bf16[64,128]{1,0:T(8,128)(2,1)S(1)}, bf16[64,128]{1,0:T(8,128)(2,1)S(1)}, u32[]{:S(2)}, u32[]{:S(2)}) collective-permute-start(bf16[64,128]{1,0:T(8,128)(2,1)S(1)} %collective-permute-done.12), channel_id=1, source_target_pairs={{0,2},{2,4},{4,6},{6,8},{8,10},{10,12},{12,14},{14,16},{16,18},{18... | collective-permute-start | bytes 49160 | tf_op jit(solution)/shard_map/ppermute | solution.py:21
  113.9 6.7 %copy-start = (f32[1024]{0:T(1024)S(1)}, f32[1024]{0:T(1024)}, u32[]{:S(2)}) copy-start(f32[1024]{0:T(1024)} %custom-call.2) | copy-start | bytes 12292
  113.9 6.7 %copy-start.2 = (f32[1024]{0:T(1024)S(1)}, f32[1024]{0:T(1024)}, u32[]{:S(2)}) copy-start(f32[1024]{0:T(1024)} %convert_multiply_fusion.1) | copy-start | bytes 12292
  140.1 10.8 %all-to-all-start = ((f32[16,2,32]{2,1,0:T(2,128)}), f32[16,2,32]{2,1,0:T(2,128)S(1)}, u32[]{:S(2)}, u32[]{:S(2)}) async-start(f32[16,2,32]{2,1,0:T(2,128)} %reshape.217), calls=%async_computation | async-start | bytes 32768 | tf_op jit(solution)/shard_map/all_to_all | solution.py:93
  154.7 10.8 %all-to-all-start.4 = ((f32[16,2,100]{2,1,0:T(2,128)}), f32[16,2,100]{2,1,0:T(2,128)S(1)}, u32[]{:S(2)}, u32[]{:S(2)}) async-start(f32[16,2,100]{2,1,0:T(2,128)} %reshape.224), calls=%async_computation.4 | async-start | bytes 32768 | tf_op jit(solution)/shard_map/all_to_all | solution.py:86
